TPU v7x, 32 devices: a whole 2x2x4 slice. The times are simulated.
32 devices in a mesh: layer: 4 (over y, x), energy: 8 (over z, core).
Axes of the slice: x: 2, y: 2, z: 4, core: 2. Of those that a mesh axis runs over, the one named last changes fastest.
Arguments:
- onsite: float32 [4, 256], P('layer'), may hold values from -1 to 1
- broadening: float32 [4, 256], P('layer'), may hold values from 1 to 2
- hamiltonian: float32 [4, 2, 256, 256], P('layer'), may hold values from -0.078125 to 0.078125
- coupling: float32 [4, 2, 256, 256], P('layer'), may hold values from -0.21875 to 0.21875
- coupling_mask: int32 [4, 256, 256], P('layer'), may hold values 0 or 1
- prior_sigma: float32 [4, 32, 2, 256, 256], P('layer', 'energy'), may hold values from -0.4 to 0.4, as said below
- kernel_weights: float32 [8], replicated, may hold values from 0.1 to 0.6
- kernel_offsets: int32 [8], replicated, may hold values from -7 to 7
Outputs:
- self_energy: float32 [4, 32, 2, 256, 256], P('layer', 'energy')
Inputs may be any that keep to these rules, and one draw needn't show every extreme that they name: `prior_sigma`: real and imaginary parts of the blocks.
All inputs are finite; a program needn't handle non-finite values. No bound on the sum of `coupling_mask` on one device may be relied on, other than what follows from the above.
Results may differ from a plain program's by a relative error of at most 0.0001.
Values sent between devices are 32-bit elements; how exact they have to be, the bound alone decides.
No kernel may reach another device: no remote copies, remote signals or barrier semaphores. Data moves between devices by JAX's collectives and lax.ppermute only.
A program may use at most 128 MiB of HBM per device.

v0:
```python
import jax
import jax.numpy as jnp
from jax import lax
from jax.sharding import PartitionSpec as P

NS_ITERS = 3
exact_mode = lax.Precision.HIGHEST


def matmul_high(first_op, second_op):
    return jnp.matmul(first_op, second_op, precision=exact_mode)


def complex_product(first_op, second_op):
    first_real = first_op[..., 0, :, :]
    first_imag = first_op[..., 1, :, :]
    second_real = second_op[..., 0, :, :]
    second_imag = second_op[..., 1, :, :]
    real_part = matmul_high(first_real, second_real) - matmul_high(first_imag, second_imag)
    imag_part = matmul_high(first_real, second_imag) + matmul_high(first_imag, second_real)
    return jnp.stack([real_part, imag_part], axis=-3)


def adjoint(matrix):
    return jnp.stack(
        [jnp.swapaxes(matrix[..., 0, :, :], -1, -2), -jnp.swapaxes(matrix[..., 1, :, :], -1, -2)],
        axis=-3,
    )


def lead_block(batch_size, orbitals):
    identity = jnp.eye(orbitals, dtype=jnp.float32)
    single = jnp.stack([jnp.zeros_like(identity), -0.5 * identity])
    return jnp.broadcast_to(single, (batch_size, 2, orbitals, orbitals))


def energy_levels(positions, grid_size):
    return -1.0 + 2.0 * (positions.astype(jnp.float32) + 0.5) / grid_size


def solve_layer(
    levels, onsite_row, damping_row, hamilton, coupler, pattern, previous, incoming, sweeps
):
    orbitals = hamilton.shape[-1]
    identity = jnp.eye(orbitals, dtype=jnp.float32)
    hermitian = 0.5 * (hamilton + adjoint(hamilton))
    masked = coupler * pattern[None]
    contact = complex_product(complex_product(masked[None], incoming), adjoint(masked)[None])
    real_diag = levels[:, None] - onsite_row[None, :]
    imag_diag = damping_row[None, :]
    shifted = jnp.stack([real_diag, imag_diag], axis=1)[..., None, :] * identity
    system = shifted - hermitian[None] - contact - previous
    diag_real = jnp.diagonal(system[:, 0], axis1=-2, axis2=-1)
    diag_imag = jnp.diagonal(system[:, 1], axis1=-2, axis2=-1)
    modulus = diag_real * diag_real + diag_imag * diag_imag
    inverse = (
        jnp.stack([diag_real / modulus, -diag_imag / modulus], axis=1)[..., None, :] * identity
    )
    for sweep_no in range(sweeps):
        residue = complex_product(system, inverse)
        inverse = 2.0 * inverse - complex_product(inverse, residue)
    return inverse


def kernel_columns(weights, offsets, row_count, column_energy):
    row_idx = jnp.arange(row_count, dtype=jnp.int32)
    matches = column_energy[None, None, :] == row_idx[None, :, None] + offsets[:, None, None]
    return jnp.sum(jnp.where(matches, weights[:, None, None], jnp.float32(0.0)), axis=0)


def solve_all_layers(gathered, previous, levels_now, orbitals, layer_count):
    incoming = lead_block(levels_now.shape[0], orbitals)
    stacked = []
    for layer_no in range(layer_count):
        incoming = solve_layer(
            levels_now,
            gathered[0][layer_no],
            gathered[1][layer_no],
            gathered[2][layer_no],
            gathered[3][layer_no],
            gathered[4][layer_no],
            previous[layer_no],
            incoming,
            NS_ITERS,
        )
        stacked.append(incoming)
    return stacked


def local(
    onsite,
    broadening,
    hamiltonian,
    coupling,
    coupling_mask,
    prior_sigma,
    kernel_weights,
    kernel_offsets,
):
    layer_count = lax.axis_size("layer")
    group_count = lax.axis_size("energy")
    per_device = prior_sigma.shape[1]
    orbitals = prior_sigma.shape[-1]
    grid_size = per_device * group_count
    sub_count = per_device // layer_count
    first_level = lax.axis_index("energy") * per_device
    own_levels = energy_levels(first_level + jnp.arange(per_device, dtype=jnp.int32), grid_size)
    gathered = (
        lax.all_gather(onsite, "layer", axis=0, tiled=True),
        lax.all_gather(broadening, "layer", axis=0, tiled=True),
        lax.all_gather(hamiltonian, "layer", axis=0, tiled=True),
        lax.all_gather(coupling, "layer", axis=0, tiled=True),
        lax.all_gather(coupling_mask.astype(jnp.float32), "layer", axis=0, tiled=True),
    )
    previous = lax.all_to_all(prior_sigma, "layer", split_axis=1, concat_axis=0, tiled=True)
    levels_now = lax.dynamic_slice_in_dim(
        own_levels, lax.axis_index("layer") * sub_count, sub_count, 0
    )
    stacked = solve_all_layers(gathered, previous, levels_now, orbitals, layer_count)
    joined = jnp.concatenate(stacked, axis=2)
    arrived = lax.all_to_all(joined, ("layer", "energy"), split_axis=2, concat_axis=0, tiled=True)
    slot = jnp.arange(arrived.shape[0], dtype=jnp.int32)
    sender_layer = slot // (group_count * sub_count)
    sender_group = slot // sub_count % group_count
    column_energy = sender_group * per_device + sender_layer * sub_count + slot % sub_count
    kernel = kernel_columns(kernel_weights, kernel_offsets, grid_size, column_energy)
    blended = jnp.einsum("fe,epij->fpij", kernel, arrived, precision=exact_mode)
    scattering = lax.all_to_all(blended, "energy", split_axis=0, concat_axis=2, tiled=True)
    return scattering[None]


def solution(mesh):
    placed = (
        P("layer", None),
        P("layer", None),
        P("layer", None, None, None),
        P("layer", None, None, None),
        P("layer", None, None),
        P("layer", "energy", None, None, None),
        P(),
        P(),
    )
    return jax.shard_map(
        local,
        mesh=mesh,
        in_specs=placed,
        out_specs=P("layer", "energy", None, None, None),
        check_vma=False,
    )
```

profile of v0, /device:TPU:0, one launch (start us, length us, event | category | flops | bytes accessed | tf_op | source)
XLA Modules:
  0.0 352.6 jit_solution(5748276882402703983)
XLA Ops:
  9.7 5.2 %all-to-all-start = ((f32[1,4,2,256,256]{4,3,2,0,1:T(8,128)}), f32[1,4,2,256,256]{4,3,2,0,1:T(8,128)}, u32[]{:S(2)}, u32[]{:S(2)}) async-start(f32[1,4,2,256,256]{4,3,2,0,1:T(8,128)} %bitcast.628), calls=%async_computation | async-start | bytes 4194304 | tf_op jit(solution)/shard_map/all_to_all | solution.py:115
  15.5 30.2 %all-gather = f32[4,1,256]{2,1,0:T(1,128)S(1)} all-gather(f32[1,1,256]{2,1,0:T(1,128)S(1)} %bitcast.645), channel_id=1, replica_groups=mesh['layer'=4,'energy'=8] {'layer'}, dimensions={0}, use_global_device_ids=true | all-gather | bytes 5120 | tf_op jit(solution)/shard_map/all_gather | solution.py:109
  45.7 8.6 %all-gather.1 = f32[4,1,256]{2,1,0:T(1,128)S(1)} all-gather(f32[1,1,256]{2,1,0:T(1,128)S(1)} %bitcast.646), channel_id=1, replica_groups=mesh['layer'=4,'energy'=8] {'layer'}, dimensions={0}, use_global_device_ids=true | all-gather | bytes 5120 | tf_op jit(solution)/shard_map/all_gather | solution.py:110
  56.4 30.5 %all-gather.8.cloned.1.call-done = f32[4,2,256,256]{3,2,1,0:T(8,128)} async-done(((f32[1,2,256,256]{3,2,1,0:T(8,128)}), f32[4,2,256,256]{3,2,1,0:T(8,128)}) %all-gather.8.cloned.1.call-update) | async-done | bytes 2097168 | tf_op jit(solution)/shard_map/all_gather | solution.py:112
  86.9 2.8 slice_multiply_fusion.3
  91.9 32.1 %all-gather.6.cloned.1.call-done = f32[4,2,256,256]{3,2,1,0:T(8,128)} async-done(((f32[1,2,256,256]{3,2,1,0:T(8,128)}), f32[4,2,256,256]{3,2,1,0:T(8,128)}) %all-gather.6.cloned.1.call-update) | async-done | bytes 2097168 | tf_op jit(solution)/shard_map/all_gather | solution.py:111
  123.9 2.8 fusion.132
  126.8 1.8 copy.76
  128.6 1.8 copy.75
  130.3 2.5 bitcast_multiply_fusion
  139.1 2.3 gather_fusion.1
  141.5 2.6 gather_fusion
  164.7 2.6 gather_fusion.3
  167.3 2.6 gather_fusion.2
  186.2 1.7 negate_bitcast_fusion.1
  191.1 2.6 gather_fusion.5
  193.7 2.6 gather_fusion.4
  215.9 2.3 gather_fusion.7
  218.3 2.3 gather_fusion.6
  230.7 2.9 copy.67
  233.6 4.8 %all-to-all-start.1 = ((f32[1,2,1024,256]{3,1,0,2:T(2,128)}), f32[1,2,1024,256]{3,1,0,2:T(2,128)S(1)}, u32[]{:S(2)}, u32[]{:S(2)}) async-start(f32[1,2,1024,256]{3,1,0,2:T(2,128)} %copy.67), calls=%async_computation.1 | async-start | bytes 4194304 | tf_op jit(solution)/shard_map/all_to_all | solution.py:121
  238.7 49.8 %all-to-all-done.1 = f32[1,2,1024,256]{3,1,0,2:T(2,128)S(1)} async-done(((f32[1,2,1024,256]{3,1,0,2:T(2,128)}), f32[1,2,1024,256]{3,1,0,2:T(2,128)S(1)}, u32[]{:S(2)}, u32[]{:S(2)}) %all-to-all-start.1) | async-done | bytes 2097184 | tf_op jit(solution)/shard_map/all_to_all | solution.py:121
  288.5 3.0 fusion
  292.7 51.5 %all_to_all.45 = f32[32,2,32,256]{3,2,1,0:T(8,128)S(1)} all-to-all(f32[32,2,32,256]{3,2,1,0:T(8,128)S(1)} %copy.70), channel_id=1, replica_groups=mesh['layer'=4,'energy'=8] {'energy'}, dimensions={0} | all-to-all | bytes 4194304 | tf_op jit(solution)/shard_map/all_to_all | solution.py:128
  (271 shorter events, 85.7 us)
Async XLA Ops:
  6.5 48.5 %all-gather.10.cloned.1.call-start = ((), (), s32[]{:S(2)}) async-start(), calls=%async_computation.5 | async-start | bytes 1310720 | tf_op jit(solution)/shard_map/all_gather | solution.py:113
  8.2 78.6 %all-gather.8.cloned.1.call-start = ((), (), s32[]{:S(2)}) async-start(), calls=%async_computation.4 | async-start | bytes 2621440 | tf_op jit(solution)/shard_map/all_gather | solution.py:112
  9.0 115.0 %all-gather.6.cloned.1.call-start = ((), (), s32[]{:S(2)}) async-start(), calls=%async_computation.3 | async-start | bytes 2621440 | tf_op jit(solution)/shard_map/all_gather | solution.py:111
  9.7 5.8 %copy-start.29 = (f32[1,256]{1,0:T(1,128)S(1)}, f32[1,256]{1,0:T(1,128)}, u32[]{:S(2)}) copy-start(f32[1,256]{1,0:T(1,128)} %param.8) | copy-start | bytes 3076
  9.7 36.0 %copy-start.30 = (f32[1,256]{1,0:T(1,128)S(1)}, f32[1,256]{1,0:T(1,128)}, u32[]{:S(2)}) copy-start(f32[1,256]{1,0:T(1,128)} %param.9) | copy-start | bytes 3076
  9.7 128.0 %all-to-all-start = ((f32[1,4,2,256,256]{4,3,2,0,1:T(8,128)}), f32[1,4,2,256,256]{4,3,2,0,1:T(8,128)}, u32[]{:S(2)}, u32[]{:S(2)}) async-start(f32[1,4,2,256,256]{4,3,2,0,1:T(8,128)} %bitcast.628), calls=%async_computation | async-start | bytes 4194304 | tf_op jit(solution)/shard_map/all_to_all | solution.py:115
  56.3 33.3 %copy-start.9 = (f32[256,256]{1,0:T(8,128)}, f32[256,256]{1,0:T(8,128)S(1)}, u32[]{:S(2)}) copy-start(f32[256,256]{1,0:T(8,128)S(1)} %get-tuple-element.21) | copy-start | bytes 786436
  56.4 33.3 %copy-start.10 = (f32[256,256]{1,0:T(8,128)}, f32[256,256]{1,0:T(8,128)S(1)}, u32[]{:S(2)}) copy-start(f32[256,256]{1,0:T(8,128)S(1)} %get-tuple-element.22) | copy-start | bytes 786436
  56.4 33.3 %copy-start.11 = (f32[256,256]{1,0:T(8,128)}, f32[256,256]{1,0:T(8,128)S(1)}, u32[]{:S(2)}) copy-start(f32[256,256]{1,0:T(8,128)S(1)} %get-tuple-element.23) | copy-start | bytes 786436
  56.4 33.3 %copy-start.12 = (f32[256,256]{1,0:T(8,128)}, f32[256,256]{1,0:T(8,128)S(1)}, u32[]{:S(2)}) copy-start(f32[256,256]{1,0:T(8,128)S(1)} %get-tuple-element.24) | copy-start | bytes 786436
  91.9 38.5 %copy-start.1 = (f32[4,2,256,256]{3,2,1,0:T(8,128)S(1)}, f32[4,2,256,256]{3,2,1,0:T(8,128)}, u32[]{:S(2)}) copy-start(f32[4,2,256,256]{3,2,1,0:T(8,128)} %all-gather.8.cloned.1.call-done) | copy-start | bytes 6291460
  134.6 3.1 copy-start.23
  134.6 3.1 copy-start
  135.0 2.8 copy-start.21
  155.5 3.5 copy-start.20
  155.9 5.6 %copy-start.19 = (f32[1,1,256,256]{3,2,1,0:T(8,128)S(1)}, f32[1,1,256,256]{3,2,1,0:T(8,128)}, u32[]{:S(2)}) copy-start(f32[1,1,256,256]{3,2,1,0:T(8,128)} %get-tuple-element.18) | copy-start | bytes 786436
  179.5 3.2 copy-start.2
  182.3 3.1 copy-start.18
  182.8 5.2 %copy-start.17 = (f32[1,1,256,256]{3,2,1,0:T(8,128)S(1)}, f32[1,1,256,256]{3,2,1,0:T(8,128)}, u32[]{:S(2)}) copy-start(f32[1,1,256,256]{3,2,1,0:T(8,128)} %get-tuple-element.16) | copy-start | bytes 786436
  207.9 3.1 copy-start.16
  208.3 5.2 %copy-start.15 = (f32[1,1,256,256]{3,2,1,0:T(8,128)S(1)}, f32[1,1,256,256]{3,2,1,0:T(8,128)}, u32[]{:S(2)}) copy-start(f32[1,1,256,256]{3,2,1,0:T(8,128)} %get-tuple-element.14) | copy-start | bytes 786436
  233.6 4.9 %copy-start.31 = (s32[8]{0:T(128)S(1)}, s32[8]{0:T(128)}, u32[]{:S(2)}) copy-start(s32[8]{0:T(128)} %param.15) | copy-start | bytes 100
  233.6 5.0 %copy-start.32 = (f32[8]{0:T(128)S(1)}, f32[8]{0:T(128)}, u32[]{:S(2)}) copy-start(f32[8]{0:T(128)} %param.14) | copy-start | bytes 100
  233.6 54.9 %all-to-all-start.1 = ((f32[1,2,1024,256]{3,1,0,2:T(2,128)}), f32[1,2,1024,256]{3,1,0,2:T(2,128)S(1)}, u32[]{:S(2)}, u32[]{:S(2)}) async-start(f32[1,2,1024,256]{3,1,0,2:T(2,128)} %copy.67), calls=%async_computation.1 | async-start | bytes 4194304 | tf_op jit(solution)/shard_map/all_to_all | solution.py:121
  (14 other events, 19.1 us)
Sparse Core Ops, SparseCore 0:
  9.2 40.0 all-gather.9
  51.1 35.6 all-gather.7
  88.7 35.1 all-gather.5
where the time goes:
time: 358 us; the launch traced here: 353 us
  waiting for transfers between devices  114 us (32%)
  blocking collectives  90.2 us (25%)
  matrix products  59.9 us (17%)
  local copies, waits for them, and re-layouts  41.3 us (12%)
  other arithmetic  22.2 us (6%)
  between operations  15.2 us (4%)
  starting transfers between devices  10.1 us (3%)
    dot_general x128, matrix products, matmul_high(): return jnp.matmul(first_op, second_op, precision=exact_mode)  56.9 us
    all_to_all x1, blocking collectives, local(): lax.all_to_all(blended, 'energy', split_axis=0, concat_axis=2, tiled=True)  51.5 us
    all_to_all x1, waiting for transfers between devices, local(): lax.all_to_all(joined, ('layer', 'energy'), split_axis=2, concat_axis=0,...  49.8 us
    all_gather x1, waiting for transfers between devices, local(): lax.all_gather(hamiltonian, 'layer', axis=0, tiled=True)  32.1 us
    all_gather x1, waiting for transfers between devices, local(): lax.all_gather(coupling, 'layer', axis=0, tiled=True)  30.5 us
    all_gather x1, blocking collectives, local(): lax.all_gather(onsite, 'layer', axis=0, tiled=True)  30.2 us
    gather x4, local copies, waits for them, and re-layouts, solve_layer(): diag_real = jnp.diagonal(system[:, 0], axis1=-2, axis2=-1)  10 us
    gather x4, local copies, waits for them, and re-layouts, solve_layer(): diag_imag = jnp.diagonal(system[:, 1], axis1=-2, axis2=-1)  9.82 us
  transfers between devices with their start and end apart: 5, of which 3 were waited for; matrix products, arithmetic and copies ran while one was open for 6% of the time, Pallas kernels for 0%

commit v1 on v0

--- a/solution.py
+++ b/solution.py
@@ -5,6 +5,12 @@
 
 NS_ITERS = 3
 exact_mode = lax.Precision.HIGHEST
+
+
+def trade_parts(x, axis, split, join):
+    cells = jnp.split(x, lax.axis_size(axis), axis=split)
+    arrived = lax.all_to_all(jnp.stack(cells), axis, 0, 0)
+    return jnp.concatenate(arrived, axis=join)
 
 
 def matmul_high(first_op, second_op):
@@ -118,7 +124,7 @@
     )
     stacked = solve_all_layers(gathered, previous, levels_now, orbitals, layer_count)
     joined = jnp.concatenate(stacked, axis=2)
-    arrived = lax.all_to_all(joined, ("layer", "energy"), split_axis=2, concat_axis=0, tiled=True)
+    arrived = trade_parts(joined, ("layer", "energy"), 2, 0)
     slot = jnp.arange(arrived.shape[0], dtype=jnp.int32)
     sender_layer = slot // (group_count * sub_count)
     sender_group = slot // sub_count % group_count

time: 358 us -> 376 us (1.050)
  local copies, waits for them, and re-layouts: 41.3 us -> 58.6 us
    unnamed x74 -> x105, local copies, waits for them, and re-layouts: 9.31 us -> 28.7 us
where the time goes in v1:
time: 376 us; the launch traced here: 370 us
  waiting for transfers between devices  114 us (30%)
  blocking collectives  90.2 us (24%)
  matrix products  59.9 us (16%)
  local copies, waits for them, and re-layouts  58.6 us (16%)
  other arithmetic  22 us (6%)
  between operations  15.3 us (4%)
  starting transfers between devices  10.2 us (3%)
    dot_general x128, matrix products, matmul_high(): return jnp.matmul(first_op, second_op, precision=exact_mode)  56.9 us
    all_to_all x1, blocking collectives, local(): lax.all_to_all(blended, 'energy', split_axis=0, concat_axis=2, tiled=True)  51.5 us
    all_to_all x1, waiting for transfers between devices, trade_parts(): arrived = lax.all_to_all(jnp.stack(cells), axis, 0, 0)  49.8 us
    all_gather x1, waiting for transfers between devices, local(): lax.all_gather(hamiltonian, 'layer', axis=0, tiled=True)  32.1 us
    all_gather x1, waiting for transfers between devices, local(): lax.all_gather(coupling, 'layer', axis=0, tiled=True)  30.5 us
    all_gather x1, blocking collectives, local(): lax.all_gather(onsite, 'layer', axis=0, tiled=True)  30.2 us
    unnamed x105, local copies, waits for them, and re-layouts  28.7 us
    gather x4, local copies, waits for them, and re-layouts, solve_layer(): diag_real = jnp.diagonal(system[:, 0], axis1=-2, axis2=-1)  10.3 us
  transfers between devices with their start and end apart: 5, of which 3 were waited for; matrix products, arithmetic and copies ran while one was open for 6% of the time, Pallas kernels for 0%

profile of v1, /device:TPU:0, one launch (start us, length us, event | category | flops | bytes accessed | tf_op | source)
XLA Modules:
  0.0 370.0 jit_solution(8681470914019702055)
XLA Ops:
  9.7 5.2 %all-to-all-start = ((f32[1,4,2,256,256]{4,3,2,0,1:T(8,128)}), f32[1,4,2,256,256]{4,3,2,0,1:T(8,128)}, u32[]{:S(2)}, u32[]{:S(2)}) async-start(f32[1,4,2,256,256]{4,3,2,0,1:T(8,128)} %bitcast.751), calls=%async_computation | async-start | bytes 4194304 | tf_op jit(solution)/shard_map/all_to_all | solution.py:121
  15.5 30.2 %all-gather = f32[4,1,256]{2,1,0:T(1,128)S(1)} all-gather(f32[1,1,256]{2,1,0:T(1,128)S(1)} %bitcast.768), channel_id=1, replica_groups=mesh['layer'=4,'energy'=8] {'layer'}, dimensions={0}, use_global_device_ids=true | all-gather | bytes 5120 | tf_op jit(solution)/shard_map/all_gather | solution.py:115
  45.7 8.6 %all-gather.1 = f32[4,1,256]{2,1,0:T(1,128)S(1)} all-gather(f32[1,1,256]{2,1,0:T(1,128)S(1)} %bitcast.769), channel_id=1, replica_groups=mesh['layer'=4,'energy'=8] {'layer'}, dimensions={0}, use_global_device_ids=true | all-gather | bytes 5120 | tf_op jit(solution)/shard_map/all_gather | solution.py:116
  56.4 30.5 %all-gather.8.cloned.1.call-done = f32[4,2,256,256]{3,2,1,0:T(8,128)} async-done(((f32[1,2,256,256]{3,2,1,0:T(8,128)}), f32[4,2,256,256]{3,2,1,0:T(8,128)}) %all-gather.8.cloned.1.call-update) | async-done | bytes 2097168 | tf_op jit(solution)/shard_map/all_gather | solution.py:118
  86.9 2.8 slice_multiply_fusion
  91.9 32.1 %all-gather.6.cloned.1.call-done = f32[4,2,256,256]{3,2,1,0:T(8,128)} async-done(((f32[1,2,256,256]{3,2,1,0:T(8,128)}), f32[4,2,256,256]{3,2,1,0:T(8,128)}) %all-gather.6.cloned.1.call-update) | async-done | bytes 2097168 | tf_op jit(solution)/shard_map/all_gather | solution.py:117
  123.9 2.9 fusion.131
  126.8 1.8 copy.55
  128.6 1.8 copy.54
  130.4 2.5 bitcast_multiply_fusion
  139.2 2.3 gather_fusion.1
  141.6 2.6 gather_fusion
  159.9 1.7 negate_bitcast_fusion.2
  164.8 2.6 gather_fusion.3
  167.3 2.6 gather_fusion.2
  186.3 1.7 negate_bitcast_fusion.1
  191.1 2.6 gather_fusion.5
  193.7 2.6 gather_fusion.4
  215.9 2.3 gather_fusion.7
  218.3 2.6 gather_fusion.6
  250.9 4.9 %all-to-all-start.1 = ((f32[32,1,2,32,256]{4,3,2,1,0:T(8,128)}), f32[32,1,2,32,256]{4,3,2,1,0:T(8,128)S(1)}, u32[]{:S(2)}, u32[]{:S(2)}) async-start(f32[32,1,2,32,256]{4,3,2,1,0:T(8,128)} %constant_dynamic-update-slice_fusion), calls=%async_computation.1 | async-start | bytes 4194304 | tf_op jit(solution)/shard_map/all_to_all | solution.py:12
  256.0 49.8 %all-to-all-done.1 = f32[32,1,2,32,256]{4,3,2,1,0:T(8,128)S(1)} async-done(((f32[32,1,2,32,256]{4,3,2,1,0:T(8,128)}), f32[32,1,2,32,256]{4,3,2,1,0:T(8,128)S(1)}, u32[]{:S(2)}, u32[]{:S(2)}) %all-to-all-start.1) | async-done | bytes 2097184 | tf_op jit(solution)/shard_map/all_to_all | solution.py:12
  305.8 3.0 fusion
  310.0 51.5 %all_to_all.32 = f32[32,2,32,256]{3,2,1,0:T(8,128)S(1)} all-to-all(f32[32,2,32,256]{3,2,1,0:T(8,128)S(1)} %copy.51), channel_id=1, replica_groups=mesh['layer'=4,'energy'=8] {'energy'}, dimensions={0} | all-to-all | bytes 4194304 | tf_op jit(solution)/shard_map/all_to_all | solution.py:134
  (301 shorter events, 103.9 us)
Async XLA Ops:
  6.5 48.5 %all-gather.10.cloned.1.call-start = ((), (), s32[]{:S(2)}) async-start(), calls=%async_computation.5 | async-start | bytes 1310720 | tf_op jit(solution)/shard_map/all_gather | solution.py:119
  8.2 78.6 %all-gather.8.cloned.1.call-start = ((), (), s32[]{:S(2)}) async-start(), calls=%async_computation.4 | async-start | bytes 2621440 | tf_op jit(solution)/shard_map/all_gather | solution.py:118
  9.0 115.0 %all-gather.6.cloned.1.call-start = ((), (), s32[]{:S(2)}) async-start(), calls=%async_computation.3 | async-start | bytes 2621440 | tf_op jit(solution)/shard_map/all_gather | solution.py:117
  9.7 5.8 %copy-start.29 = (f32[1,256]{1,0:T(1,128)S(1)}, f32[1,256]{1,0:T(1,128)}, u32[]{:S(2)}) copy-start(f32[1,256]{1,0:T(1,128)} %param.8) | copy-start | bytes 3076
  9.7 36.0 %copy-start.30 = (f32[1,256]{1,0:T(1,128)S(1)}, f32[1,256]{1,0:T(1,128)}, u32[]{:S(2)}) copy-start(f32[1,256]{1,0:T(1,128)} %param.9) | copy-start | bytes 3076
  9.7 128.0 %all-to-all-start = ((f32[1,4,2,256,256]{4,3,2,0,1:T(8,128)}), f32[1,4,2,256,256]{4,3,2,0,1:T(8,128)}, u32[]{:S(2)}, u32[]{:S(2)}) async-start(f32[1,4,2,256,256]{4,3,2,0,1:T(8,128)} %bitcast.751), calls=%async_computation | async-start | bytes 4194304 | tf_op jit(solution)/shard_map/all_to_all | solution.py:121
  56.3 33.3 %copy-start.9 = (f32[256,256]{1,0:T(8,128)}, f32[256,256]{1,0:T(8,128)S(1)}, u32[]{:S(2)}) copy-start(f32[256,256]{1,0:T(8,128)S(1)} %get-tuple-element.21) | copy-start | bytes 786436
  56.4 33.3 %copy-start.10 = (f32[256,256]{1,0:T(8,128)}, f32[256,256]{1,0:T(8,128)S(1)}, u32[]{:S(2)}) copy-start(f32[256,256]{1,0:T(8,128)S(1)} %get-tuple-element.22) | copy-start | bytes 786436
  56.4 33.3 %copy-start.11 = (f32[256,256]{1,0:T(8,128)}, f32[256,256]{1,0:T(8,128)S(1)}, u32[]{:S(2)}) copy-start(f32[256,256]{1,0:T(8,128)S(1)} %get-tuple-element.23) | copy-start | bytes 786436
  56.4 33.3 %copy-start.12 = (f32[256,256]{1,0:T(8,128)}, f32[256,256]{1,0:T(8,128)S(1)}, u32[]{:S(2)}) copy-start(f32[256,256]{1,0:T(8,128)S(1)} %get-tuple-element.24) | copy-start | bytes 786436
  91.9 38.5 %copy-start.1 = (f32[4,2,256,256]{3,2,1,0:T(8,128)S(1)}, f32[4,2,256,256]{3,2,1,0:T(8,128)}, u32[]{:S(2)}) copy-start(f32[4,2,256,256]{3,2,1,0:T(8,128)} %all-gather.8.cloned.1.call-done) | copy-start | bytes 6291460
  134.6 3.1 copy-start.23
  134.6 3.1 copy-start
  155.5 3.5 copy-start.20
  156.0 5.6 %copy-start.19 = (f32[1,1,256,256]{3,2,1,0:T(8,128)S(1)}, f32[1,1,256,256]{3,2,1,0:T(8,128)}, u32[]{:S(2)}) copy-start(f32[1,1,256,256]{3,2,1,0:T(8,128)} %get-tuple-element.17) | copy-start | bytes 786436
  179.6 3.2 copy-start.2
  182.8 5.2 %copy-start.17 = (f32[1,1,256,256]{3,2,1,0:T(8,128)S(1)}, f32[1,1,256,256]{3,2,1,0:T(8,128)}, u32[]{:S(2)}) copy-start(f32[1,1,256,256]{3,2,1,0:T(8,128)} %get-tuple-element.15) | copy-start | bytes 786436
  207.9 3.1 copy-start.16
  208.4 5.2 %copy-start.15 = (f32[1,1,256,256]{3,2,1,0:T(8,128)S(1)}, f32[1,1,256,256]{3,2,1,0:T(8,128)}, u32[]{:S(2)}) copy-start(f32[1,1,256,256]{3,2,1,0:T(8,128)} %get-tuple-element.13) | copy-start | bytes 786436
  229.9 5.6 %copy-start.3 = (f32[1,2,256,256]{3,2,1,0:T(8,128)S(1)}, f32[1,2,256,256]{3,2,1,0:T(8,128)}, u32[]{:S(2)}) copy-start(f32[1,2,256,256]{3,2,1,0:T(8,128)} %copy-done.2) | copy-start | bytes 1572868
  230.3 10.3 %copy-start.5 = (f32[1,2,256,256]{3,2,1,0:T(8,128)S(1)}, f32[1,2,256,256]{3,2,1,0:T(8,128)}, u32[]{:S(2)}) copy-start(f32[1,2,256,256]{3,2,1,0:T(8,128)} %copy-done.4) | copy-start | bytes 1572868
  250.9 4.9 %copy-start.31 = (s32[8]{0:T(128)S(1)}, s32[8]{0:T(128)}, u32[]{:S(2)}) copy-start(s32[8]{0:T(128)} %param.15) | copy-start | bytes 100
  250.9 5.0 %copy-start.32 = (f32[8]{0:T(128)S(1)}, f32[8]{0:T(128)}, u32[]{:S(2)}) copy-start(f32[8]{0:T(128)} %param.14) | copy-start | bytes 100
  250.9 54.9 %all-to-all-start.1 = ((f32[32,1,2,32,256]{4,3,2,1,0:T(8,128)}), f32[32,1,2,32,256]{4,3,2,1,0:T(8,128)S(1)}, u32[]{:S(2)}, u32[]{:S(2)}) async-start(f32[32,1,2,32,256]{4,3,2,1,0:T(8,128)} %constant_dynamic-update-slice_fusion), calls=%async_computation.1 | async-start | bytes 4194304 | tf_op jit(solution)/shard_map/all_to_all | solution.py:12
  (14 other events, 22.6 us)
Sparse Core Ops, SparseCore 0:
  9.2 40.0 all-gather.9
  51.1 35.6 all-gather.7
  88.7 35.1 all-gather.5
